TPU v7x, 512 devices: a whole 4x4x16 slice. The times are simulated.
512 devices in a mesh: head: 32 (over z, core), seq: 16 (over x, y).
Axes of the slice: x: 4, y: 4, z: 16, core: 2. Of those that a mesh axis runs over, the one named last changes fastest.
Arguments:
- queries: bfloat16 [32, 32768, 64], P('head', 'seq'), may hold values from -160 to 160
- keys: bfloat16 [32, 32768, 64], P('head', 'seq'), may hold values from -8 to 8
- values: bfloat16 [32, 32768, 64], P('head', 'seq'), may hold values from -20 to 20
- block_mask: int32 [32, 64, 256], P('head'), may hold values from 0 to 1, as said below
- block_order: int32 [64], replicated, may hold values from 0 to 63, as said below
- sparse_gain: float32 [32, 64], P('head'), may hold values from 0.1 to 1.9
- linear_gain: float32 [32, 64], P('head'), may hold values from 0.1 to 1.9
Outputs:
- mixed: float32 [32, 32768, 64], P('head', 'seq')
Inputs may be any that keep to these rules, and one draw needn't show every extreme that they name: A permutation of the query blocks; rows b * 512 to (b + 1) * 512 - 1 of queries and mixed belong to query block block_order[b]. Each row block_mask[h, n] has exactly 25 ones; at most 2 of them lie among the 16 key blocks of one index of seq, and in every row some index holds exactly 2; key block n * 4 is always selected by query block n.
All inputs are finite; a program needn't handle non-finite values.
Results may differ from a plain program's by a relative error of at most 0.002.
Values may be sent and summed in bfloat16 or wider, within the bound.
No kernel may reach another device: no remote copies, remote signals or barrier semaphores. Data moves between devices by JAX's collectives and lax.ppermute only.
A program may use at most 64 MiB of HBM per device.

v0:
```python
import jax
import jax.numpy as jnp
from jax import lax
from jax.sharding import PartitionSpec as P

BQ = 512
BK = 128


EPSILON = 1e-06
TRIPLE_PASS_MODE = lax.Precision.HIGH
NEGATIVE = -1e30


def in_blocks(x, dim, length):
    lengths = x.shape
    pieces = x.reshape(*lengths[:dim], length, lengths[dim] // length, *lengths[dim + 1 :])
    return jnp.moveaxis(pieces, dim, 0)


def summed_on_arrival(x, axis, dim):
    pieces = in_blocks(x, dim, lax.axis_size(axis))
    arrived = lax.all_to_all(pieces, axis, split_axis=0, concat_axis=0, tiled=True)
    return arrived.sum(axis=0)


def in_one_piece(arrays, axis, dim, along):
    both = jnp.concatenate(arrays, axis=along)
    result, at, done = (summed_on_arrival(both, axis, dim), 0, [])
    for a in arrays:
        done.append(lax.slice_in_dim(result, at, at + a.shape[along], axis=along))
        at += a.shape[along]
    return tuple(done)


def from_everyone(x, axis):
    copies = jnp.broadcast_to(x, (lax.axis_size(axis), *x.shape))
    return lax.all_to_all(copies, axis, split_axis=0, concat_axis=0, tiled=True)


def taken_together(x, axis):
    everything = from_everyone(x, axis)
    return jnp.sum(everything, axis=0)


def packed_total(arrays, axis):
    ravelled, at, done = (jnp.concatenate([a.reshape(-1) for a in arrays]), 0, [])
    running = taken_together(ravelled, axis)
    for a in arrays:
        done.append(running[at : at + a.size].reshape(a.shape))
        at += a.size
    return tuple(done)


def feature(values_in):
    return jax.nn.elu(values_in) + 1.0


def body(queries, keys, values, block_mask, block_order, sparse_gain, linear_gain):
    tokens_dev = queries.shape[1]
    head_width = queries.shape[2]
    seq_count = lax.axis_size("seq")
    seq_index = lax.axis_index("seq")
    query_count = tokens_dev // BQ
    key_count = tokens_dev // BK
    block_total = key_count * seq_count
    chosen_count = block_total // 10
    slot_count = max(2, chosen_count // seq_count + 1)
    score_scale = head_width ** (-0.5)
    positions = block_order.shape[0]
    order_hot = (block_order[:, None] == jnp.arange(positions, dtype=jnp.int32)[None, :]).astype(
        jnp.float32
    )
    ordered_mask = jnp.dot(order_hot, block_mask[0].astype(jnp.float32))
    own_rows = lax.dynamic_slice_in_dim(ordered_mask, seq_index * query_count, query_count, 0)
    local_cols = lax.dynamic_slice_in_dim(ordered_mask, seq_index * key_count, key_count, 1)
    query_blocks = queries[0].reshape(query_count, BQ, head_width)
    key_local = keys[0]
    value_local = values[0]
    feat_keys = feature(key_local.astype(jnp.float32)).reshape(key_count, BK, head_width)
    value_float = value_local.astype(jnp.float32).reshape(key_count, BK, head_width)
    states = jnp.einsum("jtd,jte->jde", feat_keys, value_float, precision=TRIPLE_PASS_MODE).reshape(
        key_count, head_width * head_width
    )
    key_sums = jnp.sum(feat_keys, axis=1)
    paired = jnp.concatenate([key_local, value_local], axis=1)

    def attend(block_item):
        query_block, pair_block, live_keys = block_item
        keys_block = pair_block[:, :head_width]
        values_block = pair_block[:, head_width:]
        tile_relevance = (
            jnp.einsum("qd,kd->qk", query_block, keys_block, preferred_element_type=jnp.float32)
            * score_scale
        )
        alive = live_keys[None, :] > 0.5
        tile_relevance = jnp.where(alive, tile_relevance, NEGATIVE)
        row_top = jnp.max(tile_relevance, axis=1, keepdims=True)
        weights = jnp.where(alive, jnp.exp(tile_relevance - row_top), 0.0)
        row_total = jnp.sum(weights, axis=1, keepdims=True)
        output = (
            jnp.dot(weights.astype(jnp.bfloat16), values_block, preferred_element_type=jnp.float32)
            / row_total
        )
        chosen_state = jnp.zeros((head_width * head_width,), jnp.float32)
        chosen_sum = jnp.zeros((head_width,), jnp.float32)
        return (output, chosen_state, chosen_sum)

    tile_ordinals = jnp.cumsum(local_cols, axis=1) - 1.0
    slot_ids = jnp.arange(slot_count, dtype=jnp.float32)
    picker = local_cols[:, None, :] * (tile_ordinals[:, None, :] == slot_ids[None, :, None]).astype(
        jnp.float32
    )
    flat_pairs = paired.reshape(key_count, BK * 2 * head_width)
    outgoing = jnp.dot(
        picker.reshape(positions * slot_count, key_count).astype(jnp.bfloat16),
        flat_pairs,
        preferred_element_type=jnp.float32,
    ).astype(jnp.bfloat16)
    outgoing = outgoing.reshape(seq_count, query_count, slot_count * BK, 2 * head_width)
    incoming = lax.all_to_all(outgoing, "seq", split_axis=0, concat_axis=2, tiled=True)
    pair_blocks = incoming.reshape(query_count, seq_count * slot_count * BK, 2 * head_width)
    counts = jnp.sum(own_rows.reshape(query_count, seq_count, key_count), axis=2)
    live = (slot_ids[None, None, :] < counts[:, :, None]).astype(jnp.float32)
    live_keys = jnp.broadcast_to(
        live[:, :, :, None], (query_count, seq_count, slot_count, BK)
    ).reshape(query_count, seq_count * slot_count * BK)
    sparse_blocks, chosen_states, chosen_sums = lax.map(
        attend, (query_blocks, pair_blocks, live_keys)
    )
    sparse = sparse_blocks.reshape(tokens_dev, head_width)
    unselected = 1.0 - local_cols
    partial_states = jnp.dot(unselected, states)
    partial_sums = jnp.dot(unselected, key_sums)
    remaining_states, remaining_sums = in_one_piece((partial_states, partial_sums), "seq", 0, 1)
    feature_query = feature(query_blocks.astype(jnp.float32))
    numerator = jnp.einsum(
        "svo,sol->svl",
        feature_query,
        remaining_states.reshape(query_count, head_width, head_width),
        precision=TRIPLE_PASS_MODE,
    )
    denominator = jnp.einsum(
        "ryh,rh->ry", feature_query, remaining_sums, precision=TRIPLE_PASS_MODE
    )
    linear = (numerator / denominator[:, :, None]).reshape(tokens_dev, head_width)
    square_sparse = jnp.sum(sparse * sparse, axis=1)
    square_linear = jnp.sum(linear * linear, axis=1)
    total_sparse, total_linear = packed_total((square_sparse, square_linear), "head")
    features = lax.axis_size("head") * queries.shape[0] * head_width
    rms_sparse = jnp.sqrt(total_sparse / features + EPSILON)
    rms_linear = jnp.sqrt(total_linear / features + EPSILON)
    first = sparse / rms_sparse[:, None] * sparse_gain[0][None, :]
    second = linear / rms_linear[:, None] * linear_gain[0][None, :]
    return (first + second)[None]


def solution(mesh):
    in_specs = (
        P("head", "seq", None),
        P("head", "seq", None),
        P("head", "seq", None),
        P("head", None, None),
        P(),
        P("head", None),
        P("head", None),
    )
    out_specs = P("head", "seq", None)
    return jax.shard_map(body, mesh=mesh, in_specs=in_specs, out_specs=out_specs, check_vma=False)
```

profile of v0, /device:TPU:1, one launch (start us, length us, event | category | flops | bytes accessed | tf_op | source)
XLA Modules:
  0.0 176.3 jit_solution(7722469044028082244)
XLA Ops:
  0.0 1.1 convert_bitcast_fusion
  1.2 1.0 copy.74
  3.4 1.1 fusion.42
  5.0 1.4 reshape.221
  6.4 7.6 %all-to-all-start.1 = ((f32[16,4,4160]{2,1,0:T(4,128)}), f32[16,4,4160]{2,1,0:T(4,128)S(1)}, u32[]{:S(2)}, u32[]{:S(2)}) async-start(f32[16,4,4160]{2,1,0:T(4,128)} %reshape.221), calls=%async_computation.1 | async-start | bytes 2162688 | tf_op jit(solution)/shard_map/all_to_all | solution.py:23
  14.8 3.2 %convolution_convert_fusion = bf16[128,16384]{1,0:T(8,128)(2,1)} fusion(bf16[128,16]{1,0:T(8,128)(2,1)S(1)} %bitcast.71, bf16[16,16384]{1,0:T(8,128)(2,1)S(1)} %reshape.215), kind=kOutput, calls=%fused_computation.21 | convolution fusion | flops 69206016 | bytes 4722688 | tf_op jit(solution)/shard_map/dot_general | solution.py:115
  18.0 7.5 %reshape.216 = bf16[16,4,256,128]{3,2,1,0:T(8,128)(2,1)} reshape(bf16[128,16384]{1,0:T(8,128)(2,1)} %convolution_convert_fusion) | data formatting | bytes 8388608 | tf_op jit(solution)/shard_map/reshape | solution.py:120
  25.5 3.2 %all-to-all-done.1 = f32[16,4,4160]{2,1,0:T(4,128)S(1)} async-done(((f32[16,4,4160]{2,1,0:T(4,128)}), f32[16,4,4160]{2,1,0:T(4,128)S(1)}, u32[]{:S(2)}, u32[]{:S(2)}) %all-to-all-start.1) | async-done | bytes 1064992 | tf_op jit(solution)/shard_map/all_to_all | solution.py:23
  28.6 5.4 %all-to-all-start = ((bf16[16,4,256,128]{3,2,1,0:T(8,128)(2,1)}), bf16[16,4,256,128]{3,2,1,0:T(8,128)(2,1)}, u32[]{:S(2)}, u32[]{:S(2)}) async-start(bf16[16,4,256,128]{3,2,1,0:T(8,128)(2,1)} %reshape.216), calls=%async_computation | async-start | bytes 8388608 | tf_op jit(solution)/shard_map/all_to_all | solution.py:121
  36.1 1.1 multiply_reduce_fusion
  37.2 47.3 %all-to-all-done = bf16[16,4,256,128]{3,2,1,0:T(8,128)(2,1)} async-done(((bf16[16,4,256,128]{3,2,1,0:T(8,128)(2,1)}), bf16[16,4,256,128]{3,2,1,0:T(8,128)(2,1)}, u32[]{:S(2)}, u32[]{:S(2)}) %all-to-all-start) | async-done | bytes 4194336 | tf_op jit(solution)/shard_map/all_to_all | solution.py:121
  84.6 4.6 %copy.46 = bf16[1,4,16,256,128]{4,3,2,1,0:T(8,128)(2,1)} copy(bf16[1,4,16,256,128]{4,3,1,2,0:T(8,128)(2,1)} %bitcast.9) | data formatting | bytes 8388608 | tf_op jit(solution)/shard_map/all_to_all | solution.py:121
  89.2 29.6 %while.10 = (s32[]{:T(128)}, f32[4,512,64]{1,2,0:T(8,128)S(1)}, f32[4,4096]{1,0:T(4,128)S(1)}, bf16[4,512,64]{2,1,0:T(8,128)(2,1)S(1)}, bf16[4,4096,128]{2,1,0:T(8,128)(2,1)}, /*index=5*/s32[]{:T(128)}) while((s32[]{:T(128)}, f32[4,512,64]{1,2,0:T(8,128)S(1)}, f32[4,4096]{1,0:T(4,128)S(1)}, bf16[4,512,64]{2,1,0:T(8,128)(2,1)S(1)}, ...), condition=%wide.region_5.6_spmd, body=%wide.region_2.5_spmd.sunk | while | flops 564169728 | bytes 29665364 | solution.py:128
  89.3 1.3 dynamic-slice_bitcast_fusion.2
  90.6 1.3 fusion.78
  91.9 2.6 %fusion.79 = f32[512]{0:T(512)S(1)} fusion(f32[512,4096]{1,0:T(8,128)S(1)} %get-tuple-element.82, f32[512]{0:T(512)S(1)} %get-tuple-element.83, pred[4096]{0:T(1024)(128)(4,1)S(1)} %compare_reduce_fusion.2), kind=kLoop, calls=%fused_computation.3.clone.1 | loop fusion | flops 10485248 | bytes 8396800 | tf_op jit(solution)/shard_map/while/body/eval_jaxpr/reduce_sum | solution.py:100
  94.5 2.1 %fusion.80 = f32[4,512,64]{1,2,0:T(8,128)S(1)} fusion(f32[4,512,64]{1,2,0:T(8,128)S(1)} %get-tuple-element.91, s32[]{:T(128)} %get-tuple-element.90, f32[512,4096]{1,0:T(8,128)S(1)} %get-tuple-element.82, f32[512]{0:T(512)S(1)} %get-tuple-element.83, pred[4096]{0:T(1024)(128)(4,1)S(1)} %compare_reduce_fusion.2, ...), kind=kOutput, calls=%fused_computation.9.clone.1 | convolution fusion | flops 278953984 | bytes 9576452 | tf_op jit(solution)/shard_map/while/body/eval_jaxpr/dot_general | solution.py:102
  96.7 1.3 dynamic-slice_bitcast_fusion.2
  98.0 1.3 fusion.78
  99.3 2.6 %fusion.79 = f32[512]{0:T(512)S(1)} fusion(f32[512,4096]{1,0:T(8,128)S(1)} %get-tuple-element.82, f32[512]{0:T(512)S(1)} %get-tuple-element.83, pred[4096]{0:T(1024)(128)(4,1)S(1)} %compare_reduce_fusion.2), kind=kLoop, calls=%fused_computation.3.clone.1 | loop fusion | flops 10485248 | bytes 8396800 | tf_op jit(solution)/shard_map/while/body/eval_jaxpr/reduce_sum | solution.py:100
  101.9 2.1 %fusion.80 = f32[4,512,64]{1,2,0:T(8,128)S(1)} fusion(f32[4,512,64]{1,2,0:T(8,128)S(1)} %get-tuple-element.91, s32[]{:T(128)} %get-tuple-element.90, f32[512,4096]{1,0:T(8,128)S(1)} %get-tuple-element.82, f32[512]{0:T(512)S(1)} %get-tuple-element.83, pred[4096]{0:T(1024)(128)(4,1)S(1)} %compare_reduce_fusion.2, ...), kind=kOutput, calls=%fused_computation.9.clone.1 | convolution fusion | flops 278953984 | bytes 9576452 | tf_op jit(solution)/shard_map/while/body/eval_jaxpr/dot_general | solution.py:102
  104.1 1.3 dynamic-slice_bitcast_fusion.2
  105.4 1.3 fusion.78
  106.7 2.6 %fusion.79 = f32[512]{0:T(512)S(1)} fusion(f32[512,4096]{1,0:T(8,128)S(1)} %get-tuple-element.82, f32[512]{0:T(512)S(1)} %get-tuple-element.83, pred[4096]{0:T(1024)(128)(4,1)S(1)} %compare_reduce_fusion.2), kind=kLoop, calls=%fused_computation.3.clone.1 | loop fusion | flops 10485248 | bytes 8396800 | tf_op jit(solution)/shard_map/while/body/eval_jaxpr/reduce_sum | solution.py:100
  109.3 2.1 %fusion.80 = f32[4,512,64]{1,2,0:T(8,128)S(1)} fusion(f32[4,512,64]{1,2,0:T(8,128)S(1)} %get-tuple-element.91, s32[]{:T(128)} %get-tuple-element.90, f32[512,4096]{1,0:T(8,128)S(1)} %get-tuple-element.82, f32[512]{0:T(512)S(1)} %get-tuple-element.83, pred[4096]{0:T(1024)(128)(4,1)S(1)} %compare_reduce_fusion.2, ...), kind=kOutput, calls=%fused_computation.9.clone.1 | convolution fusion | flops 278953984 | bytes 9576452 | tf_op jit(solution)/shard_map/while/body/eval_jaxpr/dot_general | solution.py:102
  111.5 1.3 dynamic-slice_bitcast_fusion.2
  112.8 1.3 fusion.78
  114.2 2.6 %fusion.79 = f32[512]{0:T(512)S(1)} fusion(f32[512,4096]{1,0:T(8,128)S(1)} %get-tuple-element.82, f32[512]{0:T(512)S(1)} %get-tuple-element.83, pred[4096]{0:T(1024)(128)(4,1)S(1)} %compare_reduce_fusion.2), kind=kLoop, calls=%fused_computation.3.clone.1 | loop fusion | flops 10485248 | bytes 8396800 | tf_op jit(solution)/shard_map/while/body/eval_jaxpr/reduce_sum | solution.py:100
  116.7 2.1 %fusion.80 = f32[4,512,64]{1,2,0:T(8,128)S(1)} fusion(f32[4,512,64]{1,2,0:T(8,128)S(1)} %get-tuple-element.91, s32[]{:T(128)} %get-tuple-element.90, f32[512,4096]{1,0:T(8,128)S(1)} %get-tuple-element.82, f32[512]{0:T(512)S(1)} %get-tuple-element.83, pred[4096]{0:T(1024)(128)(4,1)S(1)} %compare_reduce_fusion.2, ...), kind=kOutput, calls=%fused_computation.9.clone.1 | convolution fusion | flops 278953984 | bytes 9576452 | tf_op jit(solution)/shard_map/while/body/eval_jaxpr/dot_general | solution.py:102
  118.9 1.3 broadcast_in_dim.58
  120.2 21.2 %all-to-all-start.2 = ((f32[32,1,4096]{2,1,0:T(1,128)}), f32[32,1,4096]{2,1,0:T(1,128)S(1)}, u32[]{:S(2)}, u32[]{:S(2)}) async-start(f32[32,1,4096]{2,1,0:T(1,128)} %broadcast_in_dim.58), calls=%async_computation.2 | async-start | bytes 1048576 | tf_op jit(solution)/shard_map/all_to_all | solution.py:38
  142.9 32.1 %all-to-all-done.2 = f32[32,1,4096]{2,1,0:T(1,128)S(1)} async-done(((f32[32,1,4096]{2,1,0:T(1,128)}), f32[32,1,4096]{2,1,0:T(1,128)S(1)}, u32[]{:S(2)}, u32[]{:S(2)}) %all-to-all-start.2) | async-done | bytes 524320 | tf_op jit(solution)/shard_map/all_to_all | solution.py:38
  (53 shorter events, 7.7 us)
Async XLA Ops:
  0.0 14.2 %copy-start = (bf16[1,2048,64]{1,2,0:T(8,128)(2,1)S(1)}, bf16[1,2048,64]{1,2,0:T(8,128)(2,1)}, u32[]{:S(2)}) copy-start(bf16[1,2048,64]{1,2,0:T(8,128)(2,1)} %param.10) | copy-start | bytes 786436
  0.0 14.2 %copy-start.1 = (bf16[1,2048,64]{1,2,0:T(8,128)(2,1)S(1)}, bf16[1,2048,64]{1,2,0:T(8,128)(2,1)}, u32[]{:S(2)}) copy-start(bf16[1,2048,64]{1,2,0:T(8,128)(2,1)} %param.11) | copy-start | bytes 786436
  6.4 22.2 %all-to-all-start.1 = ((f32[16,4,4160]{2,1,0:T(4,128)}), f32[16,4,4160]{2,1,0:T(4,128)S(1)}, u32[]{:S(2)}, u32[]{:S(2)}) async-start(f32[16,4,4160]{2,1,0:T(4,128)} %reshape.221), calls=%async_computation.1 | async-start | bytes 2162688 | tf_op jit(solution)/shard_map/all_to_all | solution.py:23
  18.0 16.1 %copy-start.2 = (bf16[1,2048,64]{1,2,0:T(8,128)(2,1)S(1)}, bf16[1,2048,64]{1,2,0:T(8,128)(2,1)}, u32[]{:S(2)}) copy-start(bf16[1,2048,64]{1,2,0:T(8,128)(2,1)} %param.9) | copy-start | bytes 786436
  28.6 55.9 %all-to-all-start = ((bf16[16,4,256,128]{3,2,1,0:T(8,128)(2,1)}), bf16[16,4,256,128]{3,2,1,0:T(8,128)(2,1)}, u32[]{:S(2)}, u32[]{:S(2)}) async-start(bf16[16,4,256,128]{3,2,1,0:T(8,128)(2,1)} %reshape.216), calls=%async_computation | async-start | bytes 8388608 | tf_op jit(solution)/shard_map/all_to_all | solution.py:121
  89.2 86.2 %copy-start.3 = (f32[1,64]{1,0:T(1,128)S(1)}, f32[1,64]{1,0:T(1,128)}, u32[]{:S(2)}) copy-start(f32[1,64]{1,0:T(1,128)} %param.15) | copy-start | bytes 772
  89.2 86.2 %copy-start.4 = (f32[1,64]{1,0:T(1,128)S(1)}, f32[1,64]{1,0:T(1,128)}, u32[]{:S(2)}) copy-start(f32[1,64]{1,0:T(1,128)} %param.14) | copy-start | bytes 772
  120.2 54.8 %all-to-all-start.2 = ((f32[32,1,4096]{2,1,0:T(1,128)}), f32[32,1,4096]{2,1,0:T(1,128)S(1)}, u32[]{:S(2)}, u32[]{:S(2)}) async-start(f32[32,1,4096]{2,1,0:T(1,128)} %broadcast_in_dim.58), calls=%async_computation.2 | async-start | bytes 1048576 | tf_op jit(solution)/shard_map/all_to_all | solution.py:38
where the time goes:
time: 177 us; the launch traced here: 176 us
  waiting for transfers between devices  82.6 us (47%)
  starting transfers between devices  34.2 us (19%)
  local copies, waits for them, and re-layouts  24 us (14%)
  matrix products  21.1 us (12%)
  other arithmetic  14 us (8%)
    all_to_all x1, waiting for transfers between devices, body(): lax.all_to_all(outgoing, 'seq', split_axis=0, concat_axis=2, tiled=True)  47.3 us
    all_to_all x1, waiting for transfers between devices, from_everyone(): return lax.all_to_all(copies, axis, split_axis=0, concat_axis=0, tiled=True)  32.1 us
    all_to_all x1, starting transfers between devices, from_everyone(): return lax.all_to_all(copies, axis, split_axis=0, concat_axis=0, tiled=True)  21.2 us
    reduce_sum x4, other arithmetic, attend(): row_total = jnp.sum(weights, axis=1, keepdims=True)  10.2 us
    dot_general x4, matrix products, attend(): jnp.dot(weights.astype(jnp.bfloat16), values_block, preferred_element_typ...  8.46 us
    all_to_all x1, starting transfers between devices, summed_on_arrival(): lax.all_to_all(pieces, axis, split_axis=0, concat_axis=0, tiled=True)  7.58 us
    reshape x1, local copies, waits for them, and re-layouts, body(): outgoing.reshape(seq_count, query_count, slot_count * BK, 2 * head_width)  7.45 us
    all_to_all x1, starting transfers between devices, body(): lax.all_to_all(outgoing, 'seq', split_axis=0, concat_axis=2, tiled=True)  5.42 us
  transfers between devices with their start and end apart: 3, of which 3 were waited for; matrix products, arithmetic and copies ran while one was open for 9% of the time, Pallas kernels for 0%

commit v1 on v0

v1 whole, which is shorter than its diff:
```python
import functools

import jax
import jax.numpy as jnp
from jax import lax
from jax.experimental import pallas as pl
from jax.experimental.pallas import tpu as pltpu
from jax.sharding import Mesh
from jax.sharding import PartitionSpec as P

BQ = 512
BK = 128
SIDE = 4
SLOTS = 8
EPSILON = 1e-06
DEAD = 1e30
AXES = ("head", "sx", "sy")
F32 = jnp.float32
BF16 = jnp.bfloat16
VMEM = pl.BlockSpec(memory_space=pltpu.VMEM)
SMEM = pl.BlockSpec(memory_space=pltpu.SMEM)
NT = (((1,), (1,)), ((), ()))


def feature(x):
    return jnp.where(x > 0.0, x + 1.0, jnp.exp(jnp.minimum(x, 0.0)))


def thirds(x):
    a = x.astype(BF16)
    rest = x - a.astype(F32)
    b = rest.astype(BF16)
    c = (rest - b.astype(F32)).astype(BF16)
    return a, b, c


def states_kernel(un_ref, kv0, kv1, kv2, kv3, kn_ref, vt_ref, ub_ref, zb_ref, s_ref):
    width = kv0.shape[0] // 2
    per = kv0.shape[1] // BK
    total = SIDE * per
    ones = jnp.ones((16, BK), BF16)
    for g, kv in enumerate((kv0, kv1, kv2, kv3)):

        def one(jj, carry, kv=kv, g=g):
            at = pl.ds(pl.multiple_of(jj * BK, BK), BK)
            keys = kv[0:width, at]
            vals = kv[width : 2 * width, at]
            j = g * per + jj
            kn_ref[j] = keys.T
            vt_ref[j] = vals
            lhs = jnp.concatenate([vals, ones], axis=0)
            phi = feature(keys.astype(F32))
            got = None
            for piece in thirds(phi):
                part = lax.dot_general(lhs, piece, NT, preferred_element_type=F32)
                got = part if got is None else got + part
            s_ref[j] = got[0 : width + 8]
            return carry

        lax.fori_loop(0, per, one, 0, unroll=4)

    def gathered(b, carry):
        def add(j, acc):
            return acc + s_ref[j] * un_ref[b * total + j]

        acc = lax.fori_loop(0, total, add, jnp.zeros((width + 8, width), F32), unroll=8)
        state = acc[0:width]
        hi = state.astype(BF16).astype(F32)
        lo = state - hi
        ub_ref[b] = jnp.concatenate([hi, lo], axis=1).astype(BF16)
        zb_ref[b] = acc[width : width + 8]
        return carry

    lax.fori_loop(0, ub_ref.shape[0], gathered, 0)


def attend_kernel(owner, tab_ref, q_ref, kn_ref, vt_ref, ub_ref, zb_ref, o_ref, s_ref):
    width = q_ref.shape[0]
    blocks = q_ref.shape[1] // BQ
    row = lax.broadcasted_iota(jnp.int32, (16, BQ), 0)

    def step(i, carry):
        at = pl.ds(pl.multiple_of(i * BQ, BQ), BQ)
        b = owner * blocks + i
        base = b * (SLOTS + 1)
        query = q_ref[:, at] * BF16(width**-0.5)
        top = None
        for s in range(SLOTS):
            score = jnp.dot(kn_ref[tab_ref[base + s]], query, preferred_element_type=F32)
            s_ref[s * BK : (s + 1) * BK, :] = score
            part = jnp.max(score.reshape(BK // 8, 8, BQ), axis=0)
            top = part if top is None else jnp.maximum(top, part)
        top = jnp.max(top, axis=0, keepdims=True)
        count = tab_ref[base + SLOTS]
        acc = None
        total = None
        for p in range(SLOTS // 2):
            rounded = []
            for s in (2 * p, 2 * p + 1):
                shift = top + jnp.where(s < count, 0.0, DEAD).astype(F32)
                weights = jnp.exp(s_ref[s * BK : (s + 1) * BK, :] - shift)
                part = jnp.sum(weights.reshape(BK // 8, 8, BQ), axis=0)
                total = part if total is None else total + part
                rounded.append(weights.astype(BF16))
            vals = jnp.concatenate([vt_ref[tab_ref[base + 2 * p]], vt_ref[tab_ref[base + 2 * p + 1]]], axis=1)
            part = jnp.dot(vals, jnp.concatenate(rounded, axis=0), preferred_element_type=F32)
            acc = part if acc is None else acc + part
        total = jnp.sum(total, axis=0, keepdims=True)
        o_ref[0:width, at] = (acc / total).astype(BF16)
        sums = jnp.concatenate([zb_ref[b][0:1], jnp.zeros((1, BQ - width), F32)], axis=1)
        band = jnp.zeros((16, BQ), F32)
        for at_row, piece in enumerate(thirds(top) + thirds(total) + thirds(sums)):
            band = jnp.where(row == at_row, piece.astype(F32), band)
        o_ref[width : width + 16, at] = band.astype(BF16)
        for k in range(width // 16):
            lanes = pl.ds(pl.multiple_of((i * (width // 16) + k) * BK, BK), BK)
            o_ref[width + 16 : width + 32, lanes] = ub_ref[b, k * 16 : (k + 1) * 16, :]
        return carry

    lax.fori_loop(0, blocks, step, 0)


def merge_kernel(q_ref, r0, r1, r2, r3, sp_ref, li_ref, sq_ref):
    width = q_ref.shape[0]
    blocks = q_ref.shape[1] // BQ
    parts = (r0, r1, r2, r3)
    for i in range(blocks):
        at = slice(i * BQ, (i + 1) * BQ)
        tops, weights, sums = [], [], None
        for r in parts:
            band = r[width : width + 16, at].astype(F32)
            tops.append(band[0:1] + band[1:2] + band[2:3])
            weights.append(band[3:4] + band[4:5] + band[5:6])
            z = (band[6:7] + band[7:8] + band[8:9])[:, 0:BK]
            sums = z if sums is None else sums + z
        top = jnp.maximum(jnp.maximum(tops[0], tops[1]), jnp.maximum(tops[2], tops[3]))
        weights = [jnp.exp(t - top) * w for t, w in zip(tops, weights)]
        whole = (weights[0] + weights[1]) + (weights[2] + weights[3])
        sparse = None
        for r, w in zip(parts, weights):
            part = r[0:width, at].astype(F32) * (w / whole)
            sparse = part if sparse is None else sparse + part
        sp_ref[:, at] = sparse
        sq_ref[0:1, at] = jnp.sum(sparse * sparse, axis=0, keepdims=True)
        tiles = []
        for k in range(width // 16):
            lanes = slice((i * (width // 16) + k) * BK, (i * (width // 16) + k + 1) * BK)
            tile = None
            for r in parts:
                one = r[width + 16 : width + 32, lanes].astype(F32)
                tile = one if tile is None else tile + one
            tiles.append(tile)
        pair = jnp.concatenate(tiles, axis=0)
        state = pair[:, 0:width] + pair[:, width : 2 * width]
        lhs = jnp.concatenate([state, jnp.broadcast_to(sums[:, 0:width], (8, width))], axis=0)
        phi = feature(q_ref[:, at].astype(F32))
        both = jnp.dot(lhs, phi, precision=lax.Precision.HIGHEST, preferred_element_type=F32)
        linear = both[0:width] / both[width : width + 1]
        li_ref[:, at] = linear
        sq_ref[1:2, at] = jnp.sum(linear * linear, axis=0, keepdims=True)


def pairs(heads, over_rows, shift):
    out = []
    for h in range(heads):
        for x in range(SIDE):
            for y in range(SIDE):
                if (h % 2 == 0) == over_rows:
                    to = (x, (y + shift) % SIDE)
                else:
                    to = ((x + shift) % SIDE, y)
                out.append(((h * SIDE + x) * SIDE + y, (h * SIDE + to[0]) * SIDE + to[1]))
    return out


def body(heads, queries, keys, values, block_mask, block_order, sparse_gain, linear_gain):
    tokens, width = queries.shape[1], queries.shape[2]
    q_blocks, k_blocks = tokens // BQ, tokens // BK
    sx, sy = lax.axis_index("sx"), lax.axis_index("sy")
    odd = lax.axis_index("head") % 2
    own_q = jnp.swapaxes(queries[0], 0, 1)
    own_kv = jnp.concatenate([jnp.swapaxes(keys[0], 0, 1), jnp.swapaxes(values[0], 0, 1)], axis=0)
    kv = [own_kv] + [None] * 3
    qs = [own_q] + [None] * 3
    for k in (1, 3, 2):
        kv[k] = lax.ppermute(own_kv, AXES, pairs(heads, True, k))
    for k in (1, 3, 2):
        qs[k] = lax.ppermute(own_q, AXES, pairs(heads, False, k))

    back = jnp.arange(SIDE, dtype=jnp.int32)
    along_y = sx * SIDE + (sy - back) % SIDE
    along_x = ((sx - back) % SIDE) * SIDE + sy
    key_home = jnp.where(odd == 0, along_y, along_x)
    query_home = jnp.where(odd == 0, along_x, along_y)
    rows = (query_home[:, None] * q_blocks + jnp.arange(q_blocks, dtype=jnp.int32)[None, :]).reshape(-1)
    cols = (key_home[:, None] * k_blocks + jnp.arange(k_blocks, dtype=jnp.int32)[None, :]).reshape(-1)
    positions, spans = block_mask.shape[1], block_mask.shape[2]
    row_hot = (rows[:, None] == jnp.arange(positions, dtype=jnp.int32)[None, :]).astype(F32)
    order_hot = (block_order[:, None] == jnp.arange(positions, dtype=jnp.int32)[None, :]).astype(F32)
    col_hot = (jnp.arange(spans, dtype=jnp.int32)[:, None] == cols[None, :]).astype(F32)
    chosen = jnp.dot(jnp.dot(row_hot, order_hot), jnp.dot(block_mask[0].astype(F32), col_hot))
    n_cols = cols.shape[0]
    ids = jnp.arange(n_cols, dtype=jnp.int32)
    rank = jnp.dot(chosen, (ids[:, None] <= ids[None, :]).astype(F32))
    slot = jnp.arange(SLOTS, dtype=jnp.int32).astype(F32)
    hot = chosen[:, None, :] * (rank[:, None, :] == slot[None, :, None] + 1.0).astype(F32)
    table = jnp.sum(hot * ids.astype(F32)[None, None, :], axis=2)
    count = rank[:, n_cols - 1 :]
    table = jnp.where(slot[None, :] < count, table, table[:, 0:1])
    table = jnp.concatenate([table, count], axis=1).astype(jnp.int32).reshape(-1)
    unselected = (1.0 - chosen).reshape(-1)

    n_rows = rows.shape[0]
    kn, vt, ub, zb = pl.pallas_call(
        states_kernel,
        name="states",
        out_shape=(
            jax.ShapeDtypeStruct((n_cols, BK, width), BF16),
            jax.ShapeDtypeStruct((n_cols, width, BK), BF16),
            jax.ShapeDtypeStruct((n_rows, width, 2 * width), BF16),
            jax.ShapeDtypeStruct((n_rows, 8, width), F32),
        ),
        in_specs=[SMEM] + [VMEM] * 4,
        out_specs=(VMEM,) * 4,
        scratch_shapes=[pltpu.VMEM((n_cols, width + 8, width), F32)],
    )(unselected, *kv)
    parts = [None] * SIDE
    for k in (1, 3, 2, 0):
        part = pl.pallas_call(
            functools.partial(attend_kernel, k),
            name=f"attend{k}",
            out_shape=jax.ShapeDtypeStruct((width + 32, tokens), BF16),
            in_specs=[SMEM] + [VMEM] * 5,
            out_specs=VMEM,
            scratch_shapes=[pltpu.VMEM((SLOTS * BK, BQ), F32)],
        )(table, qs[k], kn, vt, ub, zb)
        parts[k] = lax.ppermute(part, AXES, pairs(heads, False, SIDE - k)) if k else part
    sparse, linear, squares = pl.pallas_call(
        merge_kernel,
        name="merge",
        out_shape=(
            jax.ShapeDtypeStruct((width, tokens), F32),
            jax.ShapeDtypeStruct((width, tokens), F32),
            jax.ShapeDtypeStruct((2, tokens), F32),
        ),
        in_specs=[VMEM] * 5,
        out_specs=(VMEM,) * 3,
    )(own_q, *parts)

    swap = [(h, h ^ 1) for h in range(heads)]
    even = odd == 0
    kept = jnp.where(even, squares[0], squares[1])
    given = jnp.where(even, squares[1], squares[0])
    mine = (kept + lax.ppermute(given, "head", swap)).reshape(-1, 128)
    ring = [[h for h in range(heads) if h % 2 == c] for c in range(2)]
    copies = jnp.broadcast_to(mine, (heads // 2, *mine.shape))
    mine = lax.all_to_all(copies, "head", 0, 0, axis_index_groups=ring, tiled=True).sum(axis=0)
    other = lax.ppermute(mine, "head", swap)
    features = heads * width
    scale = lax.rsqrt(jnp.stack([mine, other]).reshape(2, 1, tokens) / features + EPSILON)
    scale_sparse = jnp.where(even, scale[0], scale[1])
    scale_linear = jnp.where(even, scale[1], scale[0])
    mixed = sparse * scale_sparse * sparse_gain[0][:, None] + linear * scale_linear * linear_gain[0][:, None]
    return jnp.swapaxes(mixed, 0, 1)[None]


def solution(mesh):
    heads = mesh.devices.shape[0]
    grid = Mesh(mesh.devices.reshape(heads, SIDE, SIDE), AXES)
    seq = ("sx", "sy")
    in_specs = (
        P("head", seq, None),
        P("head", seq, None),
        P("head", seq, None),
        P("head", None, None),
        P(),
        P("head", None),
        P("head", None),
    )
    return jax.shard_map(
        functools.partial(body, heads), mesh=grid, in_specs=in_specs, out_specs=P("head", seq, None), check_vma=False
    )
```

time: 177 us -> 126 us (0.71)
  waiting for transfers between devices: 82.6 us -> 3.07 us
  Pallas kernels: 0 us -> 41.9 us
  blocking collectives: 0 us -> 19.8 us
  matrix products: 21.1 us -> 1.31 us
  local copies, waits for them, and re-layouts: 24 us -> 6.31 us
  starting transfers between devices: 34.2 us -> 48.1 us
  other arithmetic: 14 us -> 4.56 us
    all_to_all x3 -> x0, waiting for transfers between devices: 82.6 us -> none  [the longest x1 47.3 us: body(): lax.all_to_all(outgoing, 'seq', split_axis=0, concat_axis=2, tiled=True)]
    ppermute x0 -> x11, starting transfers between devices: none -> 48.1 us  [the longest x1 12.9 us: body(): mine = (kept + lax.ppermute(given, 'head', swap)).reshape(-1, 128)]
    pallas_call x0 -> x6, Pallas kernels: none -> 41.9 us  [the longest x4 26.1 us: body(): pl.pallas_call(functools.partial(attend_kernel, k), name=f'attend{k}', ou...]
    all_to_all x3 -> x0, starting transfers between devices: 34.2 us -> none  [the longest x1 21.2 us: from_everyone(): return lax.all_to_all(copies, axis, split_axis=0, concat_axis=0, tiled=True)]
    dot_general x15 -> x2, matrix products: 21.1 us -> 1.31 us  [the longest x1 1.18 us: body(): jnp.dot(jnp.dot(row_hot, order_hot), jnp.dot(block_mask[0].astype(F32), c...]
    all_to_all x0 -> x1, blocking collectives: none -> 19.8 us  [body(): lax.all_to_all(copies, 'head', 0, 0, axis_index_groups=ring, tiled=True)]
    reduce_sum x9 -> x2, other arithmetic: 11.3 us -> 0.19 us  [the longest x1 0.17 us: body(): table = jnp.sum(hot * ids.astype(F32)[None, None, :], axis=2)]
    reshape x9 -> x1, local copies, waits for them, and re-layouts: 10.3 us -> 0.66 us  [body(): unselected = (1.0 - chosen).reshape(-1)]
  transfers between devices with their start and end apart: 3 -> 11, of which waited for: 3 -> 3; matrix products, arithmetic and copies ran while one was open for 9% -> 3% of each run, Pallas kernels for 0% -> 31%
where the time goes in v1:
time: 126 us; the launch traced here: 125 us
  starting transfers between devices  48.1 us (38%)
  Pallas kernels  41.9 us (33%)
  blocking collectives  19.8 us (16%)
  local copies, waits for them, and re-layouts  6.31 us (5%)
  other arithmetic  4.56 us (4%)
  waiting for transfers between devices  3.07 us (2%)
  matrix products  1.31 us (1%)
    pallas_call x4, Pallas kernels, body(): pl.pallas_call(functools.partial(attend_kernel, k), name=f'attend{k}', ou...  26.1 us
    all_to_all x1, blocking collectives, body(): lax.all_to_all(copies, 'head', 0, 0, axis_index_groups=ring, tiled=True)  19.8 us
    ppermute x1, starting transfers between devices, body(): mine = (kept + lax.ppermute(given, 'head', swap)).reshape(-1, 128)  12.9 us
    pallas_call x1, Pallas kernels, body(): pl.pallas_call(states_kernel, name='states', out_shape=(jax.ShapeDtypeStr...  12.5 us
    ppermute x3, starting transfers between devices, body(): kv[k] = lax.ppermute(own_kv, AXES, pairs(heads, True, k))  11.4 us
    ppermute x3, starting transfers between devices, body(): qs[k] = lax.ppermute(own_q, AXES, pairs(heads, False, k))  10.7 us
    ppermute x3, starting transfers between devices, body(): lax.ppermute(part, AXES, pairs(heads, False, SIDE - k))  7.89 us
    ppermute x1, starting transfers between devices, body(): other = lax.ppermute(mine, 'head', swap)  5.19 us
  transfers between devices with their start and end apart: 11, of which 3 were waited for; matrix products, arithmetic and copies ran while one was open for 3% of the time, Pallas kernels for 31%

profile of v1, /device:TPU:1, one launch (start us, length us, event | category | flops | bytes accessed | tf_op | source)
XLA Modules:
  0.0 125.3 jit_solution(6241388369954151249)
XLA Ops:
  0.0 1.1 pad_maximum_fusion.kv0
  1.1 3.9 %collective-permute-start = (bf16[128,2048]{1,0:T(8,128)(2,1)S(1)}, bf16[128,2048]{1,0:T(8,128)(2,1)S(1)}, u32[]{:S(2)}, u32[]{:S(2)}) collective-permute-start(bf16[128,2048]{1,0:T(8,128)(2,1)S(1)} %pad_maximum_fusion.kv0), channel_id=1, source_target_pairs={{0,1},{1,2},{2,3},{3,0},{4,5},{5,6},{6,7},{7,4},{8,9},{9,10},{10,1... | collective-permute-start | bytes 1572872 | tf_op jit(solution)/shard_map/ppermute | solution.py:186
  5.0 4.4 %collective-permute-start.1 = (bf16[128,2048]{1,0:T(8,128)(2,1)S(1)}, bf16[128,2048]{1,0:T(8,128)(2,1)S(1)}, u32[]{:S(2)}, u32[]{:S(2)}) collective-permute-start(bf16[128,2048]{1,0:T(8,128)(2,1)S(1)} %pad_maximum_fusion.kv0), channel_id=1, source_target_pairs={{0,2},{1,3},{2,0},{3,1},{4,6},{5,7},{6,4},{7,5},{8,10},{9,11},{10,... | collective-permute-start | bytes 1572872 | tf_op jit(solution)/shard_map/ppermute | solution.py:186
  9.4 3.1 %collective-permute-start.2 = (bf16[128,2048]{1,0:T(8,128)(2,1)S(1)}, bf16[128,2048]{1,0:T(8,128)(2,1)S(1)}, u32[]{:S(2)}, u32[]{:S(2)}) collective-permute-start(bf16[128,2048]{1,0:T(8,128)(2,1)S(1)} %pad_maximum_fusion.kv0), channel_id=1, source_target_pairs={{0,3},{1,0},{2,1},{3,2},{4,7},{5,4},{6,5},{7,6},{8,11},{9,8},{10,9... | collective-permute-start | bytes 1572872 | tf_op jit(solution)/shard_map/ppermute | solution.py:186
  12.5 3.2 %collective-permute-start.3 = (bf16[64,2048]{1,0:T(8,128)(2,1)}, bf16[64,2048]{1,0:T(8,128)(2,1)S(1)}, u32[]{:S(2)}, u32[]{:S(2)}) collective-permute-start(bf16[64,2048]{1,0:T(8,128)(2,1)} %bitcast.30), channel_id=1, source_target_pairs={{0,4},{1,5},{2,6},{3,7},{4,8},{5,9},{6,10},{7,11},{8,12},{9,13},{1... | collective-permute-start | bytes 786440 | tf_op jit(solution)/shard_map/ppermute | solution.py:188
  15.7 4.5 %collective-permute-start.5 = (bf16[64,2048]{1,0:T(8,128)(2,1)}, bf16[64,2048]{1,0:T(8,128)(2,1)S(1)}, u32[]{:S(2)}, u32[]{:S(2)}) collective-permute-start(bf16[64,2048]{1,0:T(8,128)(2,1)} %bitcast.31), channel_id=1, source_target_pairs={{0,8},{1,9},{2,10},{3,11},{4,12},{5,13},{6,14},{7,15},{8,0},{9,1},... | collective-permute-start | bytes 786440 | tf_op jit(solution)/shard_map/ppermute | solution.py:188
  20.6 1.2 broadcast_subtract_fusion
  22.4 3.0 %collective-permute-start.7 = (bf16[64,2048]{1,0:T(8,128)(2,1)}, bf16[64,2048]{1,0:T(8,128)(2,1)S(1)}, u32[]{:S(2)}, u32[]{:S(2)}) collective-permute-start(bf16[64,2048]{1,0:T(8,128)(2,1)} %bitcast.32), channel_id=1, source_target_pairs={{0,12},{1,13},{2,14},{3,15},{4,0},{5,1},{6,2},{7,3},{8,4},{9,5},{1... | collective-permute-start | bytes 786440 | tf_op jit(solution)/shard_map/ppermute | solution.py:188
  25.5 0.7 convert_element_type.43.tab_ref
  26.9 0.8 copy-done.2
  27.7 0.8 copy-done.3
  28.5 12.5 %states.1 = (bf16[64,128,64]{2,1,0:T(8,128)(2,1)}, bf16[64,64,128]{2,1,0:T(8,128)(2,1)}, bf16[16,64,128]{2,1,0:T(8,128)(2,1)}, f32[16,8,64]{2,1,0:T(8,128)}) custom-call(f32[1024]{0:T(1024)} %reshape.174.un_ref, bf16[128,2048]{1,0:T(8,128)(2,1)} %copy-done, bf16[128,2048]{1,0:T(8,128)(2,1)} %copy-done.1, bf16[128,2048]{1,0:T(8,128)(2,1)} %copy-done.2, ...), custom_call_target="tpu_custom_call" | custom-call | tf_op jit(solution)/shard_map/states/pallas_call | solution.py:214
  41.0 0.7 copy-done.8
  41.8 6.5 %attend1.1 = bf16[96,2048]{1,0:T(8,128)(2,1)} custom-call(s32[144]{0:T(256)} %convert_element_type.43.tab_ref, bf16[64,2048]{1,0:T(8,128)(2,1)} %copy-done.8, bf16[64,128,64]{2,1,0:T(8,128)(2,1)} %get-tuple-element.12.kn_ref, bf16[64,64,128]{2,1,0:T(8,128)(2,1)} %get-tuple-element.13.vt_ref, bf16[16,64,128]{2,1,0:T(8,128)(2,1)} %get-tuple-element.14.ub_ref, ...), custom_call_target="tpu_custom_call" | custom-call | tf_op jit(solution)/shard_map/attend1/pallas_call | solution.py:229
  48.3 1.9 %collective-permute-start.4 = (bf16[96,2048]{1,0:T(8,128)(2,1)}, bf16[96,2048]{1,0:T(8,128)(2,1)S(1)}, u32[]{:S(2)}, u32[]{:S(2)}) collective-permute-start(bf16[96,2048]{1,0:T(8,128)(2,1)} %attend1.1), channel_id=1, source_target_pairs={{0,12},{1,13},{2,14},{3,15},{4,0},{5,1},{6,2},{7,3},{8,4},{9,5},{1... | collective-permute-start | bytes 1179656 | tf_op jit(solution)/shard_map/ppermute | solution.py:237
  50.2 0.7 copy-done.7
  50.9 6.5 %attend2.1 = bf16[96,2048]{1,0:T(8,128)(2,1)} custom-call(s32[144]{0:T(256)} %convert_element_type.43.tab_ref, bf16[64,2048]{1,0:T(8,128)(2,1)} %copy-done.7, bf16[64,128,64]{2,1,0:T(8,128)(2,1)} %get-tuple-element.12.kn_ref, bf16[64,64,128]{2,1,0:T(8,128)(2,1)} %get-tuple-element.13.vt_ref, bf16[16,64,128]{2,1,0:T(8,128)(2,1)} %get-tuple-element.14.ub_ref, ...), custom_call_target="tpu_custom_call" | custom-call | tf_op jit(solution)/shard_map/attend2/pallas_call | solution.py:229
  57.5 4.1 %collective-permute-start.6 = (bf16[96,2048]{1,0:T(8,128)(2,1)}, bf16[96,2048]{1,0:T(8,128)(2,1)S(1)}, u32[]{:S(2)}, u32[]{:S(2)}) collective-permute-start(bf16[96,2048]{1,0:T(8,128)(2,1)} %attend2.1), channel_id=1, source_target_pairs={{0,8},{1,9},{2,10},{3,11},{4,12},{5,13},{6,14},{7,15},{8,0},{9,1},... | collective-permute-start | bytes 1179656 | tf_op jit(solution)/shard_map/ppermute | solution.py:237
  61.6 0.7 copy-done.9
  62.3 6.5 %attend3.1 = bf16[96,2048]{1,0:T(8,128)(2,1)} custom-call(s32[144]{0:T(256)} %convert_element_type.43.tab_ref, bf16[64,2048]{1,0:T(8,128)(2,1)} %copy-done.9, bf16[64,128,64]{2,1,0:T(8,128)(2,1)} %get-tuple-element.12.kn_ref, bf16[64,64,128]{2,1,0:T(8,128)(2,1)} %get-tuple-element.13.vt_ref, bf16[16,64,128]{2,1,0:T(8,128)(2,1)} %get-tuple-element.14.ub_ref, ...), custom_call_target="tpu_custom_call" | custom-call | tf_op jit(solution)/shard_map/attend3/pallas_call | solution.py:229
  68.8 1.9 %collective-permute-start.8 = (bf16[96,2048]{1,0:T(8,128)(2,1)}, bf16[96,2048]{1,0:T(8,128)(2,1)S(1)}, u32[]{:S(2)}, u32[]{:S(2)}) collective-permute-start(bf16[96,2048]{1,0:T(8,128)(2,1)} %attend3.1), channel_id=1, source_target_pairs={{0,4},{1,5},{2,6},{3,7},{4,8},{5,9},{6,10},{7,11},{8,12},{9,13},{1... | collective-permute-start | bytes 1179656 | tf_op jit(solution)/shard_map/ppermute | solution.py:237
  70.7 6.5 %attend0.1.r0 = bf16[96,2048]{1,0:T(8,128)(2,1)} custom-call(s32[144]{0:T(256)} %convert_element_type.43.tab_ref, bf16[64,2048]{1,0:T(8,128)(2,1)} %bitcast.33, bf16[64,128,64]{2,1,0:T(8,128)(2,1)} %get-tuple-element.12.kn_ref, bf16[64,64,128]{2,1,0:T(8,128)(2,1)} %get-tuple-element.13.vt_ref, bf16[16,64,128]{2,1,0:T(8,128)(2,1)} %get-tuple-element.14.ub_ref, ...), custom_call_target="tpu_custom_call" | custom-call | tf_op jit(solution)/shard_map/attend0/pallas_call | solution.py:229
  77.3 1.4 %collective-permute-done.8.r3 = bf16[96,2048]{1,0:T(8,128)(2,1)S(1)} collective-permute-done((bf16[96,2048]{1,0:T(8,128)(2,1)}, bf16[96,2048]{1,0:T(8,128)(2,1)S(1)}, u32[]{:S(2)}, u32[]{:S(2)}) %collective-permute-start.8) | collective-permute-done | bytes 393248 | tf_op jit(solution)/shard_map/ppermute | solution.py:237
  78.7 0.8 copy-done.6
  79.5 3.3 %merge.1 = (f32[64,2048]{1,0:T(8,128)}, f32[64,2048]{1,0:T(8,128)}, f32[2,2048]{1,0:T(2,128)}) custom-call(bf16[64,2048]{1,0:T(8,128)(2,1)} %bitcast.34, bf16[96,2048]{1,0:T(8,128)(2,1)} %attend0.1.r0, bf16[96,2048]{1,0:T(8,128)(2,1)} %copy-done.4, bf16[96,2048]{1,0:T(8,128)(2,1)} %copy-done.5, bf16[96,2048]{1,0:T(8,128)(2,1)} %copy-done.6), custom_call_target="tpu_custom_call" | custom-call | tf_op jit(solution)/shard_map/merge/pallas_call | solution.py:238
  82.7 0.8 broadcast_select_fusion
  83.5 12.9 %collective-permute-start.9 = (f32[2048]{0:T(1024)S(1)}, f32[2048]{0:T(1024)S(1)}, u32[]{:S(2)}, u32[]{:S(2)}) collective-permute-start(f32[2048]{0:T(1024)S(1)} %bitcast.41), channel_id=1, source_target_pairs={{0,16},{16,0},{32,48},{48,32},{64,80},{80,64},{96,112},{112,96},{1... | collective-permute-start | bytes 24584 | tf_op jit(solution)/shard_map/ppermute | solution.py:254
  96.5 0.8 collective-permute-done.9
  97.3 19.8 %all_to_all.5 = f32[16,16,128]{2,1,0:T(8,128)S(1)} all-to-all(f32[16,16,128]{2,1,0:T(8,128)S(1)} %broadcast_in_dim.13), channel_id=1, replica_groups={{0,32,64,96,128,160,192,224,256,288,320,352,384,416,448,480},{16,48,80,..., dimensions={0} | all-to-all | bytes 262144 | tf_op jit(solution)/shard_map/all_to_all | solution.py:257
  117.1 5.2 %collective-permute-start.10 = (f32[16,128]{1,0:T(8,128)S(1)}, f32[16,128]{1,0:T(8,128)S(1)}, u32[]{:S(2)}, u32[]{:S(2)}) collective-permute-start(f32[16,128]{1,0:T(8,128)S(1)} %reduce_sum.19), channel_id=1, source_target_pairs={{0,16},{16,0},{32,48},{48,32},{64,80},{80,64},{96,112},{112,96},{1... | collective-permute-start | bytes 24584 | tf_op jit(solution)/shard_map/ppermute | solution.py:258
  122.3 0.8 collective-permute-done.10
  123.2 2.1 %add_bitcast_fusion = f32[1,2048,64]{1,2,0:T(8,128)} fusion(f32[64,2048]{1,0:T(8,128)} %get-tuple-element.18, f32[64,2048]{1,0:T(8,128)} %get-tuple-element.16, f32[64]{0:T(128)S(1)} %bitcast.43, f32[2048]{0:T(1024)S(1)} %bitcast.38, f32[64]{0:T(128)S(1)} %bitcast.44, f32[2048]{0:T(1024)S(1)} %bitcast.37), kind=kLoop, calls=%fused_computation.4 | loop fusion | flops 655360 | bytes 1589760 | tf_op jit(solution)/shard_map/broadcast_in_dim | solution.py:264
  (46 shorter events, 1.9 us)
Async XLA Ops:
  1.1 25.8 %copy-start = (bf16[128,2048]{1,0:T(8,128)(2,1)}, bf16[128,2048]{1,0:T(8,128)(2,1)S(1)}, u32[]{:S(2)}) copy-start(bf16[128,2048]{1,0:T(8,128)(2,1)S(1)} %pad_maximum_fusion.kv0) | copy-start | bytes 1572868
  1.1 21.3 %collective-permute-start = (bf16[128,2048]{1,0:T(8,128)(2,1)S(1)}, bf16[128,2048]{1,0:T(8,128)(2,1)S(1)}, u32[]{:S(2)}, u32[]{:S(2)}) collective-permute-start(bf16[128,2048]{1,0:T(8,128)(2,1)S(1)} %pad_maximum_fusion.kv0), channel_id=1, source_target_pairs={{0,1},{1,2},{2,3},{3,0},{4,5},{5,6},{6,7},{7,4},{8,9},{9,10},{10,1... | collective-permute-start | bytes 1572872 | tf_op jit(solution)/shard_map/ppermute | solution.py:186
  5.0 21.9 %collective-permute-start.1 = (bf16[128,2048]{1,0:T(8,128)(2,1)S(1)}, bf16[128,2048]{1,0:T(8,128)(2,1)S(1)}, u32[]{:S(2)}, u32[]{:S(2)}) collective-permute-start(bf16[128,2048]{1,0:T(8,128)(2,1)S(1)} %pad_maximum_fusion.kv0), channel_id=1, source_target_pairs={{0,2},{1,3},{2,0},{3,1},{4,6},{5,7},{6,4},{7,5},{8,10},{9,11},{10,... | collective-permute-start | bytes 1572872 | tf_op jit(solution)/shard_map/ppermute | solution.py:186
  9.4 17.5 %collective-permute-start.2 = (bf16[128,2048]{1,0:T(8,128)(2,1)S(1)}, bf16[128,2048]{1,0:T(8,128)(2,1)S(1)}, u32[]{:S(2)}, u32[]{:S(2)}) collective-permute-start(bf16[128,2048]{1,0:T(8,128)(2,1)S(1)} %pad_maximum_fusion.kv0), channel_id=1, source_target_pairs={{0,3},{1,0},{2,1},{3,2},{4,7},{5,4},{6,5},{7,6},{8,11},{9,8},{10,9... | collective-permute-start | bytes 1572872 | tf_op jit(solution)/shard_map/ppermute | solution.py:186
  12.5 28.6 %collective-permute-start.3 = (bf16[64,2048]{1,0:T(8,128)(2,1)}, bf16[64,2048]{1,0:T(8,128)(2,1)S(1)}, u32[]{:S(2)}, u32[]{:S(2)}) collective-permute-start(bf16[64,2048]{1,0:T(8,128)(2,1)} %bitcast.30), channel_id=1, source_target_pairs={{0,4},{1,5},{2,6},{3,7},{4,8},{5,9},{6,10},{7,11},{8,12},{9,13},{1... | collective-permute-start | bytes 786440 | tf_op jit(solution)/shard_map/ppermute | solution.py:188
  15.7 34.5 %collective-permute-start.5 = (bf16[64,2048]{1,0:T(8,128)(2,1)}, bf16[64,2048]{1,0:T(8,128)(2,1)S(1)}, u32[]{:S(2)}, u32[]{:S(2)}) collective-permute-start(bf16[64,2048]{1,0:T(8,128)(2,1)} %bitcast.31), channel_id=1, source_target_pairs={{0,8},{1,9},{2,10},{3,11},{4,12},{5,13},{6,14},{7,15},{8,0},{9,1},... | collective-permute-start | bytes 786440 | tf_op jit(solution)/shard_map/ppermute | solution.py:188
  22.4 4.5 %copy-start.1 = (bf16[128,2048]{1,0:T(8,128)(2,1)}, bf16[128,2048]{1,0:T(8,128)(2,1)S(1)}, u32[]{:S(2)}) copy-start(bf16[128,2048]{1,0:T(8,128)(2,1)S(1)} %collective-permute-done.kv1) | copy-start | bytes 1572868
  22.4 39.1 %collective-permute-start.7 = (bf16[64,2048]{1,0:T(8,128)(2,1)}, bf16[64,2048]{1,0:T(8,128)(2,1)S(1)}, u32[]{:S(2)}, u32[]{:S(2)}) collective-permute-start(bf16[64,2048]{1,0:T(8,128)(2,1)} %bitcast.32), channel_id=1, source_target_pairs={{0,12},{1,13},{2,14},{3,15},{4,0},{5,1},{6,2},{7,3},{8,4},{9,5},{1... | collective-permute-start | bytes 786440 | tf_op jit(solution)/shard_map/ppermute | solution.py:188
  26.9 0.8 copy-start.2
  27.7 0.8 copy-start.3
  41.0 0.7 copy-start.8
  48.3 28.9 %collective-permute-start.4 = (bf16[96,2048]{1,0:T(8,128)(2,1)}, bf16[96,2048]{1,0:T(8,128)(2,1)S(1)}, u32[]{:S(2)}, u32[]{:S(2)}) collective-permute-start(bf16[96,2048]{1,0:T(8,128)(2,1)} %attend1.1), channel_id=1, source_target_pairs={{0,12},{1,13},{2,14},{3,15},{4,0},{5,1},{6,2},{7,3},{8,4},{9,5},{1... | collective-permute-start | bytes 1179656 | tf_op jit(solution)/shard_map/ppermute | solution.py:237
  50.2 0.7 copy-start.7
  57.5 19.8 %collective-permute-start.6 = (bf16[96,2048]{1,0:T(8,128)(2,1)}, bf16[96,2048]{1,0:T(8,128)(2,1)S(1)}, u32[]{:S(2)}, u32[]{:S(2)}) collective-permute-start(bf16[96,2048]{1,0:T(8,128)(2,1)} %attend2.1), channel_id=1, source_target_pairs={{0,8},{1,9},{2,10},{3,11},{4,12},{5,13},{6,14},{7,15},{8,0},{9,1},... | collective-permute-start | bytes 1179656 | tf_op jit(solution)/shard_map/ppermute | solution.py:237
  61.5 0.7 copy-start.9
  68.8 9.9 %collective-permute-start.8 = (bf16[96,2048]{1,0:T(8,128)(2,1)}, bf16[96,2048]{1,0:T(8,128)(2,1)S(1)}, u32[]{:S(2)}, u32[]{:S(2)}) collective-permute-start(bf16[96,2048]{1,0:T(8,128)(2,1)} %attend3.1), channel_id=1, source_target_pairs={{0,4},{1,5},{2,6},{3,7},{4,8},{5,9},{6,10},{7,11},{8,12},{9,13},{1... | collective-permute-start | bytes 1179656 | tf_op jit(solution)/shard_map/ppermute | solution.py:237
  77.2 45.9 %copy-start.10 = (f32[1,64]{1,0:T(1,128)S(1)}, f32[1,64]{1,0:T(1,128)}, u32[]{:S(2)}) copy-start(f32[1,64]{1,0:T(1,128)} %param.13) | copy-start | bytes 772
  77.2 45.9 %copy-start.11 = (f32[1,64]{1,0:T(1,128)S(1)}, f32[1,64]{1,0:T(1,128)}, u32[]{:S(2)}) copy-start(f32[1,64]{1,0:T(1,128)} %param.12) | copy-start | bytes 772
  77.2 1.5 %copy-start.4 = (bf16[96,2048]{1,0:T(8,128)(2,1)}, bf16[96,2048]{1,0:T(8,128)(2,1)S(1)}, u32[]{:S(2)}) copy-start(bf16[96,2048]{1,0:T(8,128)(2,1)S(1)} %collective-permute-done.4.r1) | copy-start | bytes 1179652
  77.3 1.5 %copy-start.5 = (bf16[96,2048]{1,0:T(8,128)(2,1)}, bf16[96,2048]{1,0:T(8,128)(2,1)S(1)}, u32[]{:S(2)}) copy-start(bf16[96,2048]{1,0:T(8,128)(2,1)S(1)} %collective-permute-done.6.r2) | copy-start | bytes 1179652
  78.7 0.8 copy-start.6
  83.5 13.7 %collective-permute-start.9 = (f32[2048]{0:T(1024)S(1)}, f32[2048]{0:T(1024)S(1)}, u32[]{:S(2)}, u32[]{:S(2)}) collective-permute-start(f32[2048]{0:T(1024)S(1)} %bitcast.41), channel_id=1, source_target_pairs={{0,16},{16,0},{32,48},{48,32},{64,80},{80,64},{96,112},{112,96},{1... | collective-permute-start | bytes 24584 | tf_op jit(solution)/shard_map/ppermute | solution.py:254
  117.1 6.0 %collective-permute-start.10 = (f32[16,128]{1,0:T(8,128)S(1)}, f32[16,128]{1,0:T(8,128)S(1)}, u32[]{:S(2)}, u32[]{:S(2)}) collective-permute-start(f32[16,128]{1,0:T(8,128)S(1)} %reduce_sum.19), channel_id=1, source_target_pairs={{0,16},{16,0},{32,48},{48,32},{64,80},{80,64},{96,112},{112,96},{1... | collective-permute-start | bytes 24584 | tf_op jit(solution)/shard_map/ppermute | solution.py:258
